TPU v7x, 256 devices: a whole 4x4x8 slice. The times are simulated.
256 devices in a mesh: seq: 128 (over x, z_lo, y, core), head: 2 (over z_hi).
Axes of the slice: x: 4, y: 4, z: 8 (z_hi: 2, z_lo: 4; z = z_hi * 4 + z_lo), core: 2. Of those that a mesh axis runs over, the one named last changes fastest.
Arguments:
- queries: bfloat16 [16384, 2048], P('seq', 'head'), may hold values from -6 to 6
- keys: bfloat16 [16384, 512], P('seq', 'head'), may hold values from -6 to 6
- values: bfloat16 [16384, 512], P('seq', 'head'), may hold values from -6 to 6
- tile_mask: int32 [256, 256], replicated, may hold values from 0 to 1, as said below
- out_weight: bfloat16 [2048, 4096], P('head'), may hold values from -0.5 to 0.5
Outputs:
- mixed: bfloat16 [16384, 4096], P(('seq', 'head'))
Inputs may be any that keep to these rules, and one draw needn't show every extreme that they name: tile_mask[i, j] is 1 for i == j, 0 for j > i, and 0 or 1 below the diagonal.
All inputs are finite; a program needn't handle non-finite values.
Results may differ from a plain program's by a relative error of at most 0.01.
Values may be sent and summed in bfloat16 or wider, within the bound.
A program may use at most 128 MiB of HBM per device.

v0:
```python
import math

import jax
import jax.numpy as jnp
from jax import lax
from jax.sharding import PartitionSpec as P

HD = 128
TILE = 64


MASK_FLOOR = -1e30


def side_by_side(arrays, axis, dim, along):
    both = jnp.concatenate(arrays, axis=along)
    filled, at, finished = (lax.all_gather(both, axis, axis=dim, tiled=True), 0, [])
    for a in arrays:
        finished.append(lax.slice_in_dim(filled, at, at + a.shape[along], axis=along))
        at += a.shape[along]
    return tuple(finished)


def cut_along(shard, dim, size):
    before, after = (shard.shape[:dim], shard.shape[dim + 1 :])
    return jnp.moveaxis(shard.reshape(*before, size, -1, *after), dim, 0)


def sent_and_summed(shard, axis, dim):
    size = lax.axis_size(axis)
    parts = lax.all_to_all(cut_along(shard, dim, size), axis, 0, 0, tiled=True)
    return jnp.sum(parts.astype(jnp.float32), axis=0)


def per_device(queries, keys, values, tile_mask, out_weight):
    row_count = queries.shape[0]
    local_groups = keys.shape[1] // HD
    group = queries.shape[1] // HD // local_groups
    scale = 1.0 / math.sqrt(HD)
    seq_place = lax.axis_index("seq")
    query_index = seq_place * row_count + jnp.arange(row_count, dtype=jnp.int32)
    query_block = queries.reshape(row_count, local_groups, group, HD)
    query_tiles = query_index[::TILE] // TILE
    mask_rows = jnp.take(tile_mask, query_tiles, axis=0)

    def block_step(state, key_part, value_part, key_start):
        width = key_part.shape[0]
        key_index = key_start + jnp.arange(width, dtype=jnp.int32)
        tile_open = jnp.repeat(jnp.take(mask_rows, key_index // TILE, axis=1) > 0, TILE, axis=0)
        allowed = tile_open & (key_index[None, :] <= query_index[:, None])

        def compute(carry):
            best, total, running = carry
            allowed_wide = allowed[:, None, None, :]
            scores = (
                jnp.einsum(
                    "qgrd,kgd->qgrk",
                    query_block,
                    key_part.reshape(width, local_groups, HD),
                    preferred_element_type=jnp.float32,
                )
                * scale
            )
            masked = jnp.where(allowed_wide, scores, MASK_FLOOR)
            new_best = jnp.maximum(best, jnp.max(masked, axis=-1))
            weights = jnp.where(allowed_wide, jnp.exp(masked - new_best[..., None]), 0.0)
            rescale = jnp.exp(best - new_best)
            total = total * rescale + jnp.sum(weights, axis=-1)
            product = jnp.einsum(
                "qgrk,kgd->qgrd",
                weights.astype(jnp.bfloat16),
                value_part.reshape(width, local_groups, HD),
                preferred_element_type=jnp.float32,
            )
            running = running * rescale[..., None] + product
            return (new_best, total, running)

        def keep_state(carry):
            return carry

        return lax.cond(jnp.any(allowed), compute, keep_state, state)

    initial = (
        jnp.full((row_count, local_groups, group), MASK_FLOOR, jnp.float32),
        jnp.zeros((row_count, local_groups, group), jnp.float32),
        jnp.zeros((row_count, local_groups, group, HD), jnp.float32),
    )
    carry = initial
    key_piece, value_piece = side_by_side((keys, values), "seq", 0, 1)
    width = key_piece.shape[0]
    block_size = math.gcd(width, 2048)
    count = width // block_size
    key_blocks = key_piece.reshape(count, block_size, key_piece.shape[1])
    value_blocks = value_piece.reshape(count, block_size, value_piece.shape[1])
    offsets = block_size * jnp.arange(count, dtype=jnp.int32)

    def advance(state, item):
        key_part, value_part, key_start = item
        return (block_step(state, key_part, value_part, key_start), None)

    carry, unused = lax.scan(advance, carry, (key_blocks, value_blocks, offsets))
    best, total, running = carry
    attended = (
        (running / total[..., None])
        .reshape(row_count, local_groups * group * HD)
        .astype(jnp.bfloat16)
    )
    return sent_and_summed(
        jnp.dot(attended, out_weight, preferred_element_type=jnp.float32).astype(jnp.bfloat16),
        "head",
        0,
    ).astype(jnp.bfloat16)


def solution(mesh):
    placed = (P("seq", "head"), P("seq", "head"), P("seq", "head"), P(), P("head", None))
    return jax.shard_map(
        per_device, mesh=mesh, in_specs=placed, out_specs=P(("seq", "head"), None), check_vma=False
    )
```

profile of v0, /device:TPU:71, one launch (start us, length us, event | category | flops | bytes accessed | tf_op | source)
XLA Modules:
  0.0 453.4 jit_solution(14329220096915874139)
XLA Ops:
  10.4 213.4 %all-gather.2.cloned.1.call-done = bf16[16384,512]{1,0:T(8,128)(2,1)} async-done(((bf16[128,512]{1,0:T(8,128)(2,1)}), bf16[16384,512]{1,0:T(8,128)(2,1)}) %all-gather.2.cloned.1.call-update) | async-done | bytes 16777232 | tf_op jit(solution)/shard_map/all_gather | solution.py:17
  223.8 11.3 %fusion.21 = (bf16[16384,256]{1,0:T(8,128)(2,1)}, bf16[16384,256]{1,0:T(8,128)(2,1)}) fusion(bf16[16384,512]{1,0:T(8,128)(2,1)} %all-gather.2.cloned.1.call-done), kind=kLoop, calls=%fused_computation.54 | loop fusion | bytes 33554432 | tf_op jit(solution)/shard_map/slice | solution.py:19
  235.1 11.5 %copy.24 = bf16[8,2048,256]{1,2,0:T(8,128)(2,1)} copy(bf16[8,2048,256]{2,1,0:T(8,128)(2,1)} %bitcast.59) | data formatting | bytes 16777216
  246.6 11.4 %copy.26 = bf16[8,2048,256]{1,2,0:T(8,128)(2,1)} copy(bf16[8,2048,256]{2,1,0:T(8,128)(2,1)} %bitcast.58) | data formatting | bytes 16777216
  258.1 156.5 %while.17 = (s32[]{:T(128)}, f32[128,2,4]{0,2,1:T(4,128)S(1)}, f32[128,2,4]{0,2,1:T(4,128)S(1)}, f32[128,2,4,128]{3,0,2,1:T(8,128)S(1)}, s32[8]{0:T(128)S(1)}, /...) while((s32[]{:T(128)}, f32[128,2,4]{0,2,1:T(4,128)S(1)}, ...), condition=%wide.region_6.7_spmd.clone, body=%wide.region_0.6_spmd.clone.sunk | while | flops 1102676096 | bytes 35064600 | solution.py:101
  259.4 5.5 %gather_fusion = s32[2048,2]{1,0:T(8,128)S(1)} fusion(s32[2,256]{0,1:T(8,128)S(1)} %get-tuple-element.423, s32[2048]{0:T(1024)S(1)} %broadcast_clamp_fusion.2), kind=kCustom, calls=%fused_computation.clone.clone.1 | custom fusion | bytes 40960 | tf_op jit(solution)/shard_map/while/body/eval_jaxpr/jit(_take)/gather | solution.py:49
  268.7 8.9 %conditional.3 = ((f32[128,2,4]{0,2,1:T(4,128)S(1)}, f32[128,2,4]{0,2,1:T(4,128)S(1)}, f32[128,2,4,128]{3,0,2,1:T(8,128)S(1)})) conditional(s32[]{:T(128)} %convert_element_type.35, (f32[128,2,4]{0,2,1:T(4,128)S(1)}, f32[128,2,4]{0,2,1:T(4,128)S(1)}, f32[128,2,4,128]{3,0,2,1:T(8,128)S(1)}) %tuple.55, (pred[2,64,2048]{2,1,0:T(8,128)(4,1)S(1)}, ...), branch_computations={%region_2.2_spmd, %region_3.5_spmd} | conditional | flops 1101793280 | bytes 34677284 | solution.py:81
  272.7 2.0 fusion.4
  274.8 2.9 fusion.11
  279.0 5.5 %gather_fusion = s32[2048,2]{1,0:T(8,128)S(1)} fusion(s32[2,256]{0,1:T(8,128)S(1)} %get-tuple-element.423, s32[2048]{0:T(1024)S(1)} %broadcast_clamp_fusion.2), kind=kCustom, calls=%fused_computation.clone.clone.1 | custom fusion | bytes 40960 | tf_op jit(solution)/shard_map/while/body/eval_jaxpr/jit(_take)/gather | solution.py:49
  288.3 8.9 %conditional.3 = ((f32[128,2,4]{0,2,1:T(4,128)S(1)}, f32[128,2,4]{0,2,1:T(4,128)S(1)}, f32[128,2,4,128]{3,0,2,1:T(8,128)S(1)})) conditional(s32[]{:T(128)} %convert_element_type.35, (f32[128,2,4]{0,2,1:T(4,128)S(1)}, f32[128,2,4]{0,2,1:T(4,128)S(1)}, f32[128,2,4,128]{3,0,2,1:T(8,128)S(1)}) %tuple.55, (pred[2,64,2048]{2,1,0:T(8,128)(4,1)S(1)}, ...), branch_computations={%region_2.2_spmd, %region_3.5_spmd} | conditional | flops 1101793280 | bytes 34677284 | solution.py:81
  294.3 2.9 fusion.11
  298.5 5.5 %gather_fusion = s32[2048,2]{1,0:T(8,128)S(1)} fusion(s32[2,256]{0,1:T(8,128)S(1)} %get-tuple-element.423, s32[2048]{0:T(1024)S(1)} %broadcast_clamp_fusion.2), kind=kCustom, calls=%fused_computation.clone.clone.1 | custom fusion | bytes 40960 | tf_op jit(solution)/shard_map/while/body/eval_jaxpr/jit(_take)/gather | solution.py:49
  307.8 8.9 %conditional.3 = ((f32[128,2,4]{0,2,1:T(4,128)S(1)}, f32[128,2,4]{0,2,1:T(4,128)S(1)}, f32[128,2,4,128]{3,0,2,1:T(8,128)S(1)})) conditional(s32[]{:T(128)} %convert_element_type.35, (f32[128,2,4]{0,2,1:T(4,128)S(1)}, f32[128,2,4]{0,2,1:T(4,128)S(1)}, f32[128,2,4,128]{3,0,2,1:T(8,128)S(1)}) %tuple.55, (pred[2,64,2048]{2,1,0:T(8,128)(4,1)S(1)}, ...), branch_computations={%region_2.2_spmd, %region_3.5_spmd} | conditional | flops 1101793280 | bytes 34677284 | solution.py:81
  313.9 2.9 fusion.11
  318.1 5.5 %gather_fusion = s32[2048,2]{1,0:T(8,128)S(1)} fusion(s32[2,256]{0,1:T(8,128)S(1)} %get-tuple-element.423, s32[2048]{0:T(1024)S(1)} %broadcast_clamp_fusion.2), kind=kCustom, calls=%fused_computation.clone.clone.1 | custom fusion | bytes 40960 | tf_op jit(solution)/shard_map/while/body/eval_jaxpr/jit(_take)/gather | solution.py:49
  327.4 8.9 %conditional.3 = ((f32[128,2,4]{0,2,1:T(4,128)S(1)}, f32[128,2,4]{0,2,1:T(4,128)S(1)}, f32[128,2,4,128]{3,0,2,1:T(8,128)S(1)})) conditional(s32[]{:T(128)} %convert_element_type.35, (f32[128,2,4]{0,2,1:T(4,128)S(1)}, f32[128,2,4]{0,2,1:T(4,128)S(1)}, f32[128,2,4,128]{3,0,2,1:T(8,128)S(1)}) %tuple.55, (pred[2,64,2048]{2,1,0:T(8,128)(4,1)S(1)}, ...), branch_computations={%region_2.2_spmd, %region_3.5_spmd} | conditional | flops 1101793280 | bytes 34677284 | solution.py:81
  333.5 2.9 fusion.11
  337.6 5.5 %gather_fusion = s32[2048,2]{1,0:T(8,128)S(1)} fusion(s32[2,256]{0,1:T(8,128)S(1)} %get-tuple-element.423, s32[2048]{0:T(1024)S(1)} %broadcast_clamp_fusion.2), kind=kCustom, calls=%fused_computation.clone.clone.1 | custom fusion | bytes 40960 | tf_op jit(solution)/shard_map/while/body/eval_jaxpr/jit(_take)/gather | solution.py:49
  347.0 8.9 %conditional.3 = ((f32[128,2,4]{0,2,1:T(4,128)S(1)}, f32[128,2,4]{0,2,1:T(4,128)S(1)}, f32[128,2,4,128]{3,0,2,1:T(8,128)S(1)})) conditional(s32[]{:T(128)} %convert_element_type.35, (f32[128,2,4]{0,2,1:T(4,128)S(1)}, f32[128,2,4]{0,2,1:T(4,128)S(1)}, f32[128,2,4,128]{3,0,2,1:T(8,128)S(1)}) %tuple.55, (pred[2,64,2048]{2,1,0:T(8,128)(4,1)S(1)}, ...), branch_computations={%region_2.2_spmd, %region_3.5_spmd} | conditional | flops 1101793280 | bytes 34677284 | solution.py:81
  353.0 2.9 fusion.11
  357.2 5.5 %gather_fusion = s32[2048,2]{1,0:T(8,128)S(1)} fusion(s32[2,256]{0,1:T(8,128)S(1)} %get-tuple-element.423, s32[2048]{0:T(1024)S(1)} %broadcast_clamp_fusion.2), kind=kCustom, calls=%fused_computation.clone.clone.1 | custom fusion | bytes 40960 | tf_op jit(solution)/shard_map/while/body/eval_jaxpr/jit(_take)/gather | solution.py:49
  366.5 8.9 %conditional.3 = ((f32[128,2,4]{0,2,1:T(4,128)S(1)}, f32[128,2,4]{0,2,1:T(4,128)S(1)}, f32[128,2,4,128]{3,0,2,1:T(8,128)S(1)})) conditional(s32[]{:T(128)} %convert_element_type.35, (f32[128,2,4]{0,2,1:T(4,128)S(1)}, f32[128,2,4]{0,2,1:T(4,128)S(1)}, f32[128,2,4,128]{3,0,2,1:T(8,128)S(1)}) %tuple.55, (pred[2,64,2048]{2,1,0:T(8,128)(4,1)S(1)}, ...), branch_computations={%region_2.2_spmd, %region_3.5_spmd} | conditional | flops 1101793280 | bytes 34677284 | solution.py:81
  372.6 2.9 fusion.11
  376.8 5.5 %gather_fusion = s32[2048,2]{1,0:T(8,128)S(1)} fusion(s32[2,256]{0,1:T(8,128)S(1)} %get-tuple-element.423, s32[2048]{0:T(1024)S(1)} %broadcast_clamp_fusion.2), kind=kCustom, calls=%fused_computation.clone.clone.1 | custom fusion | bytes 40960 | tf_op jit(solution)/shard_map/while/body/eval_jaxpr/jit(_take)/gather | solution.py:49
  386.1 8.9 %conditional.3 = ((f32[128,2,4]{0,2,1:T(4,128)S(1)}, f32[128,2,4]{0,2,1:T(4,128)S(1)}, f32[128,2,4,128]{3,0,2,1:T(8,128)S(1)})) conditional(s32[]{:T(128)} %convert_element_type.35, (f32[128,2,4]{0,2,1:T(4,128)S(1)}, f32[128,2,4]{0,2,1:T(4,128)S(1)}, f32[128,2,4,128]{3,0,2,1:T(8,128)S(1)}) %tuple.55, (pred[2,64,2048]{2,1,0:T(8,128)(4,1)S(1)}, ...), branch_computations={%region_2.2_spmd, %region_3.5_spmd} | conditional | flops 1101793280 | bytes 34677284 | solution.py:81
  392.2 2.9 fusion.11
  396.3 5.5 %gather_fusion = s32[2048,2]{1,0:T(8,128)S(1)} fusion(s32[2,256]{0,1:T(8,128)S(1)} %get-tuple-element.423, s32[2048]{0:T(1024)S(1)} %broadcast_clamp_fusion.2), kind=kCustom, calls=%fused_computation.clone.clone.1 | custom fusion | bytes 40960 | tf_op jit(solution)/shard_map/while/body/eval_jaxpr/jit(_take)/gather | solution.py:49
  405.7 8.9 %conditional.3 = ((f32[128,2,4]{0,2,1:T(4,128)S(1)}, f32[128,2,4]{0,2,1:T(4,128)S(1)}, f32[128,2,4,128]{3,0,2,1:T(8,128)S(1)})) conditional(s32[]{:T(128)} %convert_element_type.35, (f32[128,2,4]{0,2,1:T(4,128)S(1)}, f32[128,2,4]{0,2,1:T(4,128)S(1)}, f32[128,2,4,128]{3,0,2,1:T(8,128)S(1)}) %tuple.55, (pred[2,64,2048]{2,1,0:T(8,128)(4,1)S(1)}, ...), branch_computations={%region_2.2_spmd, %region_3.5_spmd} | conditional | flops 1101793280 | bytes 34677284 | solution.py:81
  411.7 2.9 fusion.11
  414.9 4.7 %convolution_convert_fusion = bf16[128,4096]{1,0:T(8,128)(2,1)S(1)} fusion(bf16[128,1024]{0,1:T(8,128)(2,1)S(1)} %bitcast.63, bf16[1024,4096]{1,0:T(8,128)(2,1)} %param.13), kind=kOutput, calls=%fused_computation.41 | convolution fusion | flops 1074266112 | bytes 9699328 | tf_op jit(solution)/shard_map/dot_general | solution.py:109
  419.6 25.8 %all_to_all.5 = bf16[2,64,4096]{2,1,0:T(8,128)(2,1)S(1)} all-to-all(bf16[2,64,4096]{2,1,0:T(8,128)(2,1)S(1)} %bitcast.61), channel_id=1, replica_groups=mesh['seq'=128,'head'=2] {'head'}, dimensions={0} | all-to-all | bytes 2097152 | tf_op jit(solution)/shard_map/all_to_all | solution.py:31
  (174 shorter events, 86.7 us)
Async XLA Ops:
  6.5 1.8 copy-start
  6.5 217.3 %all-gather.2.cloned.1.call-start = ((), (), s32[]{:S(2)}) async-start(), calls=%async_computation.1 | async-start | bytes 16908288 | tf_op jit(solution)/shard_map/all_gather | solution.py:17
  414.9 31.7 %copy-start.1 = (s32[256,256]{1,0:T(8,128)S(1)}, s32[256,256]{1,0:T(8,128)}, u32[]{:S(2)}) copy-start(s32[256,256]{1,0:T(8,128)} %param.12) | copy-start | bytes 786436
Sparse Core Ops, SparseCore 0:
  9.2 214.5 all-gather.1
where the time goes:
time: 455 us; the launch traced here: 453 us
  waiting for transfers between devices  213 us (47%)
  local copies, waits for them, and re-layouts  107 us (24%)
  other arithmetic  47.9 us (11%)
  matrix products  39.7 us (9%)
  blocking collectives  25.8 us (6%)
  between operations  13.5 us (3%)
  loops' own time  6.45 us (1%)
    all_gather x1, waiting for transfers between devices, side_by_side(): lax.all_gather(both, axis, axis=dim, tiled=True)  213 us
    gather x8, local copies, waits for them, and re-layouts, block_step(): jnp.take(mask_rows, key_index // TILE, axis=1) > 0  43.7 us
    all_to_all x1, blocking collectives, sent_and_summed(): parts = lax.all_to_all(cut_along(shard, dim, size), axis, 0, 0, tiled=True)  25.8 us
    unnamed x9, local copies, waits for them, and re-layouts  24.3 us
    dot_general x8, matrix products, compute(): jnp.einsum('qgrk,kgd->qgrd', weights.astype(jnp.bfloat16), value_part.res...  22.8 us
    dynamic_slice x16, local copies, waits for them, and re-layouts, per_device(): lax.scan(advance, carry, (key_blocks, value_blocks, offsets))  18.6 us
    reduce_sum x8, other arithmetic, compute(): total = total * rescale + jnp.sum(weights, axis=-1)  16.1 us
    dot_general x8, matrix products, compute(): jnp.einsum('qgrd,kgd->qgrk', query_block, key_part.reshape(width, local_g...  12.1 us
  transfers between devices with their start and end apart: 1, of which 1 were waited for; matrix products, arithmetic and copies ran while one was open for 0% of the time, Pallas kernels for 0%

commit v1 on v0

v1 whole, which is shorter than its diff:
```python
import math

import jax
import jax.numpy as jnp
from jax import lax
from jax.experimental import pallas as pl
from jax.experimental.pallas import tpu as pltpu
from jax.sharding import PartitionSpec as P

HD = 128
MESH = pl.DeviceIdType.MESH
OFF = -1e30
FLOOR = -1e6
EXP_SCALE = math.log2(math.e) / math.sqrt(HD)
COLS = 512


def kernel(q_hbm, k_hbm, v_hbm, mask_hbm, w_hbm, out_ref,
           buf, qs, w, mask8, bias, dbias, mx, ls, acc, att, osend, pown, psend, precv,
           lsem, qlsem, wsem, msem, zs, zr, qss, qsr, a_s, a_r, b_s, b_r, d_s, d_r, o_s, o_r, p_s, p_r):
    s = lax.axis_index("seq")
    h = lax.axis_index("head")
    c = s % 2
    y = (s // 2) % 4
    z = (s // 8) % 4
    x = s // 32
    a = y * (1 - c) + x * c
    b = x * (1 - c) + y * c
    g = z % 2
    chip = x * 16 + z * 4 + y
    pair_z = z + 1 - 2 * g
    pair_chip = (3 - x) * 16 + pair_z * 4 + y

    def dev(xx, zz, yy, cc, hh):
        return {"seq": ((xx * 4 + zz) * 4 + yy) * 2 + cc, "head": hh}

    def a_dev(d):
        return dev((x + c * d + 4) % 4, z, (y + (1 - c) * d + 4) % 4, c, h)

    def b_dev(d):
        return dev((x + (1 - c) * d + 4) % 4, z, (y + c * d + 4) % 4, c, h)

    def z_of(k):
        return ((z // 2 + k // 2) % 2) * 2 + (z % 2 + k % 2) % 2

    mate = dev(x, z, y, 1 - c, h)
    pair = dev(3 - x, pair_z, y, c, h)
    across = dev(x, z, y, c, 1 - h)

    def remote(src, dst, ss, rs, to):
        return pltpu.make_async_remote_copy(
            src_ref=src, dst_ref=dst, send_sem=ss, recv_sem=rs, device_id=to, device_id_type=MESH)

    def cols(start, size):
        return pl.ds(pl.multiple_of(start, 128), size)

    locals_ = [
        pltpu.make_async_copy(k_hbm.at[:, cols(g * 128, 128)], buf.at[c, b, z, 0, a], lsem.at[0]),
        pltpu.make_async_copy(v_hbm.at[:, cols(g * 128, 128)], buf.at[c, b, z, 1, a], lsem.at[1]),
    ]
    qlocals = [
        pltpu.make_async_copy(q_hbm.at[:, cols(g * 512 + i * 128, 128)], qs.at[0, i], qlsem.at[i])
        for i in range(4)
    ]
    mask_own = pltpu.make_async_copy(
        mask_hbm.at[pl.ds(pl.multiple_of((chip // 2) * 8, 8), 8)], mask8.at[0], msem.at[0])
    mask_pair = pltpu.make_async_copy(
        mask_hbm.at[pl.ds(pl.multiple_of((pair_chip // 2) * 8, 8), 8)], mask8.at[1], msem.at[1])
    for cp in locals_:
        cp.start()

    barrier = pltpu.get_barrier_semaphore()
    friends = [a_dev(1), a_dev(-1), b_dev(1), b_dev(-1), mate, pair, across] + [
        dev(x, z_of(k), y, c, h) for k in (1, 2, 3)]
    for f in friends:
        pl.semaphore_signal(barrier, inc=1, device_id=f, device_id_type=MESH)
    mask_own.start()
    mask_pair.start()
    for cp in qlocals:
        cp.start()
    pl.semaphore_wait(barrier, len(friends))

    def z_copy(k, t):
        src = k_hbm if t == 0 else v_hbm
        zt = z_of(k)
        return remote(src.at[:, cols((zt % 2) * 128, 128)], buf.at[c, b, z, t, a],
                      zs.at[k, t], zr.at[k, t], dev(x, zt, y, c, h))

    def q_copy(i):
        return remote(q_hbm.at[:, cols((1 - g) * 512 + i * 128, 128)], qs.at[1, i],
                      qss.at[i], qsr.at[i], pair)

    def a_copy(k, way):
        zt = z_of(k)
        if way == 0:
            ref, to = buf.at[c, b, zt, :, a], a_dev(1)
        elif way == 1:
            ref, to = buf.at[c, b, zt, :, a], a_dev(-1)
        elif way == 2:
            ref, to = buf.at[c, b, zt, 0, (a + 3) % 4], a_dev(1)
        else:
            ref, to = buf.at[c, b, zt, 1, (a + 1) % 4], a_dev(-1)
        return remote(ref, ref, a_s.at[k, way], a_r.at[k, way], to)

    def b_copy(k, way):
        zt = z_of(k)
        if way == 0:
            ref, to = buf.at[c, b, zt], b_dev(1)
        elif way == 1:
            ref, to = buf.at[c, b, zt], b_dev(-1)
        elif way == 2:
            ref, to = buf.at[c, (b + 3) % 4, zt, 0], b_dev(1)
        else:
            ref, to = buf.at[c, (b + 1) % 4, zt, 1], b_dev(-1)
        return remote(ref, ref, b_s.at[k, way], b_r.at[k, way], to)

    def unit_of(base, i):
        return (base + (4 - i) * (i % 2) * (1 - i // 2) + (i // 2) * (1 + i % 2)) % 4

    def d_copy(k, i):
        ref = buf.at[c, unit_of(b, i), z_of(k)]
        return remote(ref, ref, d_s.at[k, i], d_r.at[k, i], mate)

    for k in (1, 2, 3):
        for t in range(2):
            z_copy(k, t).start()
    for i in range(4):
        q_copy(i).start()
    for cp in locals_:
        cp.wait()
    a_copy(0, 0).start()
    a_copy(0, 1).start()
    wcopy = pltpu.make_async_copy(w_hbm, w, wsem)
    wcopy.start()

    mask_own.wait()
    mask_pair.wait()
    lane = lax.broadcasted_iota(jnp.int32, (8, 128), 1)
    for r, row_chip in ((0, chip), (1, pair_chip)):
        at = (row_chip % 2) * 2 + c
        all8 = mask8[r]
        two = jnp.where(at < 2, jnp.where(at == 0, all8[0:2], all8[2:4]),
                        jnp.where(at == 2, all8[4:6], all8[6:8]))
        rows8 = jnp.concatenate([two] * 4, axis=0)
        open8 = jnp.where(rows8 > 0, 0.0, OFF).astype(jnp.float32)
        for blk in range(128):
            first = jnp.broadcast_to(open8[:, 2 * blk:2 * blk + 1], (8, 128))
            second = jnp.broadcast_to(open8[:, 2 * blk + 1:2 * blk + 2], (8, 128))
            bias[r, blk] = jnp.where(lane < 64, first, second)
        own_blk = row_chip * 2 + c
        dbias[r] = bias[r, own_blk]
        bias[r, own_blk] = jnp.full((8, 128), OFF, jnp.float32)

    mx[...] = jnp.full(mx.shape, FLOOR, jnp.float32)
    ls[...] = jnp.zeros(ls.shape, jnp.float32)
    acc[...] = jnp.zeros(acc.shape, jnp.float32)

    def update(r, scores, vals):
        old = mx[r]
        best = jnp.max(scores, axis=1, keepdims=True)
        new = jnp.maximum(old, best)
        probs = jnp.exp2((scores - new[:, :1]) * EXP_SCALE)
        shrink = jnp.exp2((old - new) * EXP_SCALE)
        part = probs[:, 0:128]
        for j in range(1, probs.shape[1] // 128):
            part = part + probs[:, j * 128:(j + 1) * 128]
        ls[r] = ls[r] * shrink + part
        acc[r] = acc[r] * shrink + jnp.dot(
            probs.astype(jnp.bfloat16), vals, preferred_element_type=jnp.float32)
        mx[r] = new

    def spread(rows):
        two = [jnp.broadcast_to(rows[t:t + 1], (64, rows.shape[1])) for t in range(2)]
        one = jnp.concatenate(two, axis=0)
        return jnp.concatenate([one] * 4, axis=0)

    def attend(st, bb, zz, r):
        low_chip = (1 - st) * (bb * 16 + zz * 4) + st * (zz * 4 + bb)
        row_chip = chip * (1 - r) + pair_chip * r

        @pl.when(low_chip <= row_chip)
        def _():
            keys = buf[st, bb, zz, 0].reshape(512, HD)
            vals = buf[st, bb, zz, 1].reshape(512, HD)
            scores = lax.dot_general(qs[r].reshape(512, HD), keys, (((1,), (1,)), ((), ())),
                                     preferred_element_type=jnp.float32)
            rows = []
            for i in range(4):
                at = ((1 - st) * (bb * 16 + zz * 4 + i) + st * (i * 16 + zz * 4 + bb)) * 2 + st
                rows.append(bias[r, at][0:2])
            update(r, scores + spread(jnp.concatenate(rows, axis=1)), vals)

    def diagonal(r, carry):
        zz = z * (1 - r) + pair_z * r
        xx = x * (1 - r) + (3 - x) * r
        aa = y * (1 - c) + xx * c
        bb = xx * (1 - c) + y * c
        keys = buf[c, bb, zz, 0, aa]
        vals = buf[c, bb, zz, 1, aa]
        scores = lax.dot_general(qs[r].reshape(512, HD), keys, (((1,), (1,)), ((), ())),
                                 preferred_element_type=jnp.float32)
        row = lax.broadcasted_iota(jnp.int32, (512, 128), 0) % 128
        col = lax.broadcasted_iota(jnp.int32, (512, 128), 1)
        rows = dbias[r][0:2]
        scores = jnp.where(col <= row, scores + spread(rows), OFF)
        update(r, scores, vals)
        return carry

    def stream_units(k, first, count):
        def body(t, carry):
            other = t // (2 * count)
            i = first + (t // 2) % count
            r = t % 2

            @pl.when((other == 1) & (r == 0))
            def _():
                d_copy(k, i).wait_recv()

            st = c * (1 - other) + (1 - c) * other
            base = b * (1 - other) + a * other
            attend(st, unit_of(base, i), z_of(k), r)
            return carry

        lax.fori_loop(0, 4 * count, body, 0)

    def a_forward(k):
        a_copy(k, 0).wait_recv()
        a_copy(k, 2).start()
        a_copy(k, 1).wait_recv()
        a_copy(k, 3).start()

    def a_begin(k):
        z_copy(k, 0).wait_recv()
        z_copy(k, 1).wait_recv()
        a_copy(k, 0).start()
        a_copy(k, 1).start()

    def b_begin(k):
        a_copy(k, 2).wait_recv()
        a_copy(k, 3).wait_recv()
        b_copy(k, 0).start()
        b_copy(k, 1).start()
        d_copy(k, 0).start()

    a_forward(0)
    a_begin(1)
    b_begin(0)
    a_forward(1)
    a_begin(2)
    b_begin(1)
    a_forward(2)
    a_begin(3)
    b_begin(2)
    a_forward(3)
    b_begin(3)
    for cp in qlocals:
        cp.wait()
    for i in range(4):
        q_copy(i).wait()

    def own_units(k, carry):
        stream_units(k, 0, 1)
        return carry

    lax.fori_loop(0, 4, own_units, 0)

    def near_units(k, carry):
        b_copy(k, 0).wait_recv()
        b_copy(k, 2).start()
        b_copy(k, 1).wait_recv()
        b_copy(k, 3).start()
        d_copy(k, 1).start()
        d_copy(k, 2).start()
        stream_units(k, 1, 2)
        return carry

    lax.fori_loop(0, 4, near_units, 0)
    lax.fori_loop(0, 2, diagonal, 0)

    def far_units(k, carry):
        b_copy(k, 2).wait_recv()
        b_copy(k, 3).wait_recv()
        d_copy(k, 3).start()
        stream_units(k, 3, 1)
        return carry

    lax.fori_loop(0, 4, far_units, 0)

    def result(r):
        total = jnp.sum(ls[r], axis=1, keepdims=True)
        done = (acc[r] / total).astype(jnp.bfloat16)
        return jnp.concatenate([done[i * 128:(i + 1) * 128] for i in range(4)], axis=1)

    osend[...] = result(1)
    o_copy = remote(osend, att.at[g], o_s, o_r, pair)
    o_copy.start()
    att[g] = result(0)
    wcopy.wait()
    o_copy.wait()

    def p_copy(n):
        return remote(psend.at[n], precv.at[n], p_s.at[n], p_r.at[n], across)

    def project(n, carry):
        at = cols(n * COLS, COLS)
        part = jnp.dot(att[0], w[0:512, at], preferred_element_type=jnp.float32)
        part = part + jnp.dot(att[1], w[512:1024, at], preferred_element_type=jnp.float32)
        upper, lower = part[0:64], part[64:128]
        mine = jnp.where(h == 0, upper, lower)
        theirs = jnp.where(h == 0, lower, upper)
        psend[n] = theirs.astype(jnp.bfloat16)
        p_copy(n).start()
        pown[n] = mine
        return carry

    lax.fori_loop(0, 4096 // COLS, project, 0)

    def finish(n, carry):
        p_copy(n).wait()
        out_ref[:, cols(n * COLS, COLS)] = (pown[n] + precv[n].astype(jnp.float32)).astype(jnp.bfloat16)
        return carry

    lax.fori_loop(0, 4096 // COLS, finish, 0)

    def drain(k, carry):
        for way in range(4):
            a_copy(k, way).wait_send()
            b_copy(k, way).wait_send()
        for i in range(4):
            d_copy(k, i).wait_send()
        return carry

    lax.fori_loop(0, 4, drain, 0)
    for k in (1, 2, 3):
        for t in range(2):
            z_copy(k, t).wait_send()


def per_device(queries, keys, values, tile_mask, out_weight):
    dma = pltpu.SemaphoreType.DMA
    bf, f32 = jnp.bfloat16, jnp.float32
    n = 4096 // COLS
    return pl.pallas_call(
        kernel,
        out_shape=jax.ShapeDtypeStruct((64, 4096), bf),
        in_specs=[pl.BlockSpec(memory_space=pltpu.HBM)] * 5,
        out_specs=pl.BlockSpec(memory_space=pltpu.VMEM),
        scratch_shapes=[
            pltpu.VMEM((2, 4, 4, 2, 4, 128, 128), bf),
            pltpu.VMEM((2, 4, 128, 128), bf),
            pltpu.VMEM((1024, 4096), bf),
            pltpu.VMEM((2, 8, 256), jnp.int32),
            pltpu.VMEM((2, 128, 8, 128), f32),
            pltpu.VMEM((2, 8, 128), f32),
            pltpu.VMEM((2, 512, 128), f32),
            pltpu.VMEM((2, 512, 128), f32),
            pltpu.VMEM((2, 512, 128), f32),
            pltpu.VMEM((2, 128, 512), bf),
            pltpu.VMEM((128, 512), bf),
            pltpu.VMEM((n, 64, COLS), f32),
            pltpu.VMEM((n, 64, COLS), bf),
            pltpu.VMEM((n, 64, COLS), bf),
            dma((2,)), dma((4,)), dma, dma((2,)),
            dma((4, 2)), dma((4, 2)), dma((4,)), dma((4,)),
            dma((4, 4)), dma((4, 4)), dma((4, 4)), dma((4, 4)), dma((4, 4)), dma((4, 4)),
            dma, dma, dma((n,)), dma((n,)),
        ],
        compiler_params=pltpu.CompilerParams(
            collective_id=0, has_side_effects=True, vmem_limit_bytes=48 * 1024 * 1024),
    )(queries, keys, values, tile_mask, out_weight)


def solution(mesh):
    placed = (P("seq", "head"), P("seq", "head"), P("seq", "head"), P(), P("head", None))
    return jax.shard_map(
        per_device, mesh=mesh, in_specs=placed, out_specs=P(("seq", "head"), None), check_vma=False
    )
```

time: 455 us -> 113 us (0.25)
  waiting for transfers between devices: 213 us -> 0 us
  Pallas kernels: 0 us -> 107 us
  local copies, waits for them, and re-layouts: 107 us -> 4.37 us
  other arithmetic: 47.9 us -> 0 us
  matrix products: 39.7 us -> 0 us
  blocking collectives: 25.8 us -> 0 us
  between operations: 13.5 us -> 0.01 us
  loops' own time: 6.45 us -> 0 us
    all_gather x1 -> x0, waiting for transfers between devices: 213 us -> none  [side_by_side(): lax.all_gather(both, axis, axis=dim, tiled=True)]
    pallas_call x0 -> x1, Pallas kernels: none -> 107 us  [per_device(): pl.pallas_call(kernel, out_shape=jax.ShapeDtypeStruct((64, 4096), bf), in...]
    gather x9 -> x0, local copies, waits for them, and re-layouts: 44.3 us -> none  [the longest x8 43.7 us: block_step(): jnp.take(mask_rows, key_index // TILE, axis=1) > 0]
    dot_general x17 -> x0, matrix products: 39.7 us -> none  [the longest x8 22.8 us: compute(): jnp.einsum('qgrk,kgd->qgrd', weights.astype(jnp.bfloat16), value_part.res...]
    all_to_all x1 -> x0, blocking collectives: 25.8 us -> none  [sent_and_summed(): parts = lax.all_to_all(cut_along(shard, dim, size), axis, 0, 0, tiled=True)]
    unnamed x9, local copies, waits for them, and re-layouts: 24.3 us -> 4.37 us
    dynamic_slice x16 -> x0, local copies, waits for them, and re-layouts: 18.6 us -> none  [per_device(): lax.scan(advance, carry, (key_blocks, value_blocks, offsets))]
    reduce_sum x9 -> x0, other arithmetic: 17.2 us -> none  [the longest x8 16.1 us: compute(): total = total * rescale + jnp.sum(weights, axis=-1)]
  transfers between devices with their start and end apart: 1 -> 0, of which waited for: 1 -> 0; matrix products, arithmetic and copies ran while one was open for 0% -> 0% of each run, Pallas kernels for 0% -> 0%
where the time goes in v1:
time: 113 us; the launch traced here: 111 us
  Pallas kernels  107 us (95%)
  local copies, waits for them, and re-layouts  4.37 us (4%)
    pallas_call x1, Pallas kernels, per_device(): pl.pallas_call(kernel, out_shape=jax.ShapeDtypeStruct((64, 4096), bf), in...  107 us
    unnamed x9, local copies, waits for them, and re-layouts  4.37 us

profile of v1, /device:TPU:71, one launch (start us, length us, event | category | flops | bytes accessed | tf_op | source)
XLA Modules:
  0.0 111.1 jit_solution(16410108124678327425)
XLA Ops:
  0.0 0.0 copy-start
  0.0 0.9 copy-done
  1.0 0.0 copy-start.1
  1.0 0.9 copy-done.1
  1.9 0.0 copy-start.2
  1.9 0.8 copy-done.2
  2.7 0.0 copy-start.3
  2.7 0.8 copy-done.3
  3.6 106.7 %shard_map.55 = bf16[64,4096]{1,0:T(8,128)(2,1)S(1)} custom-call(bf16[128,1024]{1,0:T(8,128)(2,1)S(1)} %copy-done, bf16[128,256]{1,0:T(8,128)(2,1)S(1)} %copy-done.2, bf16[128,256]{1,0:T(8,128)(2,1)S(1)} %copy-done.3, s32[256,256]{1,0:T(8,128)S(1)} %copy-done.1, bf16[1024,4096]{1,0:T(8,128)(2,1)} %w_hbm.1), custom_call_target="tpu_custom_call" | custom-call | tf_op jit(solution)/shard_map/pallas_call | solution.py:343
  110.3 0.8 copy.7
Async XLA Ops:
  0.0 0.9 copy-start
  1.0 0.9 copy-start.1
  1.9 0.8 copy-start.2
  2.7 0.8 copy-start.3

commit v2 on v1

--- a/solution.py
+++ b/solution.py
@@ -16,7 +16,7 @@
 
 
 def kernel(q_hbm, k_hbm, v_hbm, mask_hbm, w_hbm, out_ref,
-           buf, qs, w, mask8, bias, dbias, mx, ls, acc, att, osend, pown, psend, precv,
+           buf, qs, w, mask8, bias, dbias, mx, ls, acc, sbuf, att, osend, pown, psend, precv,
            lsem, qlsem, wsem, msem, zs, zr, qss, qsr, a_s, a_r, b_s, b_r, d_s, d_r, o_s, o_r, p_s, p_r):
     s = lax.axis_index("seq")
     h = lax.axis_index("head")
@@ -135,93 +135,110 @@
 
     mask_own.wait()
     mask_pair.wait()
-    lane = lax.broadcasted_iota(jnp.int32, (8, 128), 1)
     for r, row_chip in ((0, chip), (1, pair_chip)):
         at = (row_chip % 2) * 2 + c
         all8 = mask8[r]
         two = jnp.where(at < 2, jnp.where(at == 0, all8[0:2], all8[2:4]),
                         jnp.where(at == 2, all8[4:6], all8[6:8]))
-        rows8 = jnp.concatenate([two] * 4, axis=0)
-        open8 = jnp.where(rows8 > 0, 0.0, OFF).astype(jnp.float32)
-        for blk in range(128):
-            first = jnp.broadcast_to(open8[:, 2 * blk:2 * blk + 1], (8, 128))
-            second = jnp.broadcast_to(open8[:, 2 * blk + 1:2 * blk + 2], (8, 128))
-            bias[r, blk] = jnp.where(lane < 64, first, second)
-        own_blk = row_chip * 2 + c
-        dbias[r] = bias[r, own_blk]
-        bias[r, own_blk] = jnp.full((8, 128), OFF, jnp.float32)
+        open2 = jnp.where(two > 0, 0.0, OFF).astype(jnp.float32)
+        wide = jnp.concatenate([jnp.broadcast_to(open2[i:i + 1], (64, 256)) for i in range(2)], axis=0)
+        bias[r] = jnp.transpose(wide).reshape(256, 1, 128)
+        for i in range(2):
+            own_tile = (row_chip * 2 + c) * 2 + i
+            dbias[r, i] = bias[r, own_tile]
+            bias[r, own_tile] = jnp.full((1, 128), OFF, jnp.float32)
 
     mx[...] = jnp.full(mx.shape, FLOOR, jnp.float32)
     ls[...] = jnp.zeros(ls.shape, jnp.float32)
     acc[...] = jnp.zeros(acc.shape, jnp.float32)
 
-    def update(r, scores, vals):
+    def masked(scores, r, rows):
+        tiles = [jnp.broadcast_to(jnp.concatenate([row] * 4, axis=1), (64, 512)) for row in rows]
+        return scores + jnp.concatenate(tiles, axis=0)
+
+    def dot_keys(keys, r):
+        return lax.dot_general(keys, qs[r].reshape(512, HD), (((1,), (1,)), ((), ())),
+                               preferred_element_type=jnp.float32)
+
+    def soften(r, scores, best):
         old = mx[r]
-        best = jnp.max(scores, axis=1, keepdims=True)
         new = jnp.maximum(old, best)
-        probs = jnp.exp2((scores - new[:, :1]) * EXP_SCALE)
+        probs = jnp.exp2((scores - new) * EXP_SCALE)
         shrink = jnp.exp2((old - new) * EXP_SCALE)
-        part = probs[:, 0:128]
-        for j in range(1, probs.shape[1] // 128):
-            part = part + probs[:, j * 128:(j + 1) * 128]
-        ls[r] = ls[r] * shrink + part
-        acc[r] = acc[r] * shrink + jnp.dot(
-            probs.astype(jnp.bfloat16), vals, preferred_element_type=jnp.float32)
+        ls[r] = ls[r] * shrink + jnp.sum(probs, axis=0, keepdims=True)
         mx[r] = new
-
-    def spread(rows):
-        two = [jnp.broadcast_to(rows[t:t + 1], (64, rows.shape[1])) for t in range(2)]
-        one = jnp.concatenate(two, axis=0)
-        return jnp.concatenate([one] * 4, axis=0)
-
-    def attend(st, bb, zz, r):
-        low_chip = (1 - st) * (bb * 16 + zz * 4) + st * (zz * 4 + bb)
-        row_chip = chip * (1 - r) + pair_chip * r
-
-        @pl.when(low_chip <= row_chip)
+        return probs.astype(jnp.bfloat16), shrink
+
+    def blend(r, probs, shrink, vals):
+        acc[r] = acc[r] * shrink + lax.dot_general(
+            vals, probs, (((0,), (0,)), ((), ())), preferred_element_type=jnp.float32)
+
+    def first_chip(st, bb, zz):
+        return (1 - st) * (bb * 16 + zz * 4) + st * (zz * 4 + bb)
+
+    def score_job(job):
+        st, bb, zz, r = job
+        rows = []
+        for i in range(4):
+            tile = (((1 - st) * (bb * 16 + zz * 4 + i) + st * (i * 16 + zz * 4 + bb)) * 2 + st) * 2
+            rows += [bias[r, tile], bias[r, tile + 1]]
+        scores = masked(dot_keys(buf[st, bb, zz, 0].reshape(512, HD), r), r, rows)
+        sbuf[...] = scores
+        return jnp.max(scores, axis=0, keepdims=True)
+
+    def run(ks, units, streams):
+        count = len(ks) * len(units) * len(streams) * 2
+
+        def pick(values, at):
+            out = values[0]
+            for i in range(1, len(values)):
+                out = jnp.where(at == i, values[i], out)
+            return out
+
+        def job_at(n):
+            r = n % 2
+            other = pick(streams, (n // 2) % len(streams))
+            i = pick(units, (n // 2 // len(streams)) % len(units))
+            k = pick(ks, n // 2 // len(streams) // len(units))
+            st = c * (1 - other) + (1 - c) * other
+            return st, unit_of(b * (1 - other) + a * other, i), z_of(k), r
+
+        ends, total = [], 0
+        for n in range(count):
+            st, bb, zz, r = job_at(n)
+            row_chip = chip * (1 - r) + pair_chip * r
+            total = total + jnp.where(first_chip(st, bb, zz) <= row_chip, 1, 0)
+            ends.append(total)
+
+        def nth(t):
+            n = 0
+            for end in ends[:-1]:
+                n = n + jnp.where(end <= t, 1, 0)
+            return job_at(n)
+
+        @pl.when(total > 0)
         def _():
-            keys = buf[st, bb, zz, 0].reshape(512, HD)
-            vals = buf[st, bb, zz, 1].reshape(512, HD)
-            scores = lax.dot_general(qs[r].reshape(512, HD), keys, (((1,), (1,)), ((), ())),
-                                     preferred_element_type=jnp.float32)
-            rows = []
-            for i in range(4):
-                at = ((1 - st) * (bb * 16 + zz * 4 + i) + st * (i * 16 + zz * 4 + bb)) * 2 + st
-                rows.append(bias[r, at][0:2])
-            update(r, scores + spread(jnp.concatenate(rows, axis=1)), vals)
+            def body(t, best):
+                st, bb, zz, r = nth(t)
+                probs, shrink = soften(r, sbuf[...], best)
+                following = score_job(nth(jnp.minimum(t + 1, total - 1)))
+                blend(r, probs, shrink, buf[st, bb, zz, 1].reshape(512, HD))
+                return following
+
+            lax.fori_loop(0, total, body, score_job(nth(0)))
 
     def diagonal(r, carry):
         zz = z * (1 - r) + pair_z * r
         xx = x * (1 - r) + (3 - x) * r
         aa = y * (1 - c) + xx * c
         bb = xx * (1 - c) + y * c
-        keys = buf[c, bb, zz, 0, aa]
-        vals = buf[c, bb, zz, 1, aa]
-        scores = lax.dot_general(qs[r].reshape(512, HD), keys, (((1,), (1,)), ((), ())),
-                                 preferred_element_type=jnp.float32)
-        row = lax.broadcasted_iota(jnp.int32, (512, 128), 0) % 128
-        col = lax.broadcasted_iota(jnp.int32, (512, 128), 1)
-        rows = dbias[r][0:2]
-        scores = jnp.where(col <= row, scores + spread(rows), OFF)
-        update(r, scores, vals)
+        scores = masked(dot_keys(buf[c, bb, zz, 0, aa], r), r, [dbias[r, 0], dbias[r, 1]])
+        key = lax.broadcasted_iota(jnp.int32, (128, 512), 0)
+        row = lax.broadcasted_iota(jnp.int32, (128, 512), 1) % 128
+        scores = jnp.where(key <= row, scores, OFF)
+        probs, shrink = soften(r, scores, jnp.max(scores, axis=0, keepdims=True))
+        blend(r, probs, shrink, buf[c, bb, zz, 1, aa])
         return carry
-
-    def stream_units(k, first, count):
-        def body(t, carry):
-            other = t // (2 * count)
-            i = first + (t // 2) % count
-            r = t % 2
-
-            @pl.when((other == 1) & (r == 0))
-            def _():
-                d_copy(k, i).wait_recv()
-
-            st = c * (1 - other) + (1 - c) * other
-            base = b * (1 - other) + a * other
-            attend(st, unit_of(base, i), z_of(k), r)
-            return carry
-
-        lax.fori_loop(0, 4 * count, body, 0)
 
     def a_forward(k):
         a_copy(k, 0).wait_recv()
@@ -241,6 +258,23 @@
         b_copy(k, 0).start()
         b_copy(k, 1).start()
         d_copy(k, 0).start()
+
+    def d_arrived(*pairs):
+        for k, i in pairs:
+            d_copy(k, i).wait_recv()
+
+    def near(k):
+        b_copy(k, 0).wait_recv()
+        b_copy(k, 2).start()
+        b_copy(k, 1).wait_recv()
+        b_copy(k, 3).start()
+        d_copy(k, 1).start()
+        d_copy(k, 2).start()
+
+    def far(k):
+        b_copy(k, 2).wait_recv()
+        b_copy(k, 3).wait_recv()
+        d_copy(k, 3).start()
 
     a_forward(0)
     a_begin(1)
@@ -251,50 +285,47 @@
     a_forward(2)
     a_begin(3)
     b_begin(2)
-    a_forward(3)
-    b_begin(3)
     for cp in qlocals:
         cp.wait()
     for i in range(4):
         q_copy(i).wait()
-
-    def own_units(k, carry):
-        stream_units(k, 0, 1)
-        return carry
-
-    lax.fori_loop(0, 4, own_units, 0)
-
-    def near_units(k, carry):
-        b_copy(k, 0).wait_recv()
-        b_copy(k, 2).start()
-        b_copy(k, 1).wait_recv()
-        b_copy(k, 3).start()
-        d_copy(k, 1).start()
-        d_copy(k, 2).start()
-        stream_units(k, 1, 2)
-        return carry
-
-    lax.fori_loop(0, 4, near_units, 0)
+    a_forward(3)
+    b_begin(3)
+    run((0, 1, 2), (0,), (0,))
+    d_arrived((0, 0), (1, 0), (2, 0), (3, 0))
+    near(0)
+    run((0, 1, 2), (0,), (1,))
+    near(1)
+    run((3,), (0,), (0, 1))
+    near(2)
+    d_arrived((0, 1), (0, 2), (1, 1), (1, 2))
+    run((0, 1), (1, 2), (0, 1))
+    near(3)
+    far(0)
+    d_arrived((2, 1), (2, 2))
+    run((2,), (1, 2), (0, 1))
+    far(1)
+    d_arrived((3, 1), (3, 2), (0, 3))
+    run((3,), (1, 2), (0, 1))
     lax.fori_loop(0, 2, diagonal, 0)
-
-    def far_units(k, carry):
-        b_copy(k, 2).wait_recv()
-        b_copy(k, 3).wait_recv()
-        d_copy(k, 3).start()
-        stream_units(k, 3, 1)
-        return carry
-
-    lax.fori_loop(0, 4, far_units, 0)
+    far(2)
+    d_arrived((1, 3))
+    run((0, 1), (3,), (0, 1))
+    far(3)
+    run((2, 3), (3,), (0,))
+    d_arrived((2, 3), (3, 3))
+    run((2, 3), (3,), (1,))
 
     def result(r):
-        total = jnp.sum(ls[r], axis=1, keepdims=True)
-        done = (acc[r] / total).astype(jnp.bfloat16)
-        return jnp.concatenate([done[i * 128:(i + 1) * 128] for i in range(4)], axis=1)
-
-    osend[...] = result(1)
+        done = acc[r] / ls[r]
+        return [jnp.transpose(done[:, i * 128:(i + 1) * 128]).astype(jnp.bfloat16) for i in range(4)]
+
+    for i, part in enumerate(result(1)):
+        osend[:, i * 128:(i + 1) * 128] = part
     o_copy = remote(osend, att.at[g], o_s, o_r, pair)
     o_copy.start()
-    att[g] = result(0)
+    for i, part in enumerate(result(0)):
+        att[g, :, i * 128:(i + 1) * 128] = part
     wcopy.wait()
     o_copy.wait()
 
@@ -350,11 +381,12 @@
             pltpu.VMEM((2, 4, 128, 128), bf),
             pltpu.VMEM((1024, 4096), bf),
             pltpu.VMEM((2, 8, 256), jnp.int32),
-            pltpu.VMEM((2, 128, 8, 128), f32),
-            pltpu.VMEM((2, 8, 128), f32),
-            pltpu.VMEM((2, 512, 128), f32),
-            pltpu.VMEM((2, 512, 128), f32),
-            pltpu.VMEM((2, 512, 128), f32),
+            pltpu.VMEM((2, 256, 1, 128), f32),
+            pltpu.VMEM((2, 2, 1, 128), f32),
+            pltpu.VMEM((2, 1, 512), f32),
+            pltpu.VMEM((2, 1, 512), f32),
+            pltpu.VMEM((2, 128, 512), f32),
+            pltpu.VMEM((512, 512), f32),
             pltpu.VMEM((2, 128, 512), bf),
             pltpu.VMEM((128, 512), bf),
             pltpu.VMEM((n, 64, COLS), f32),

time: 113 us -> 91.4 us (0.81)
  the two profiles are of different devices: /device:TPU:71 before, /device:TPU:67 now
where the time goes in v2:
time: 91.4 us; the launch traced here: 91.2 us
  Pallas kernels  86.8 us (95%)
  local copies, waits for them, and re-layouts  4.37 us (5%)
    pallas_call x1, Pallas kernels, per_device(): pl.pallas_call(kernel, out_shape=jax.ShapeDtypeStruct((64, 4096), bf), in...  86.8 us
    unnamed x9, local copies, waits for them, and re-layouts  4.37 us

profile of v2, /device:TPU:67, one launch (start us, length us, event | category | flops | bytes accessed | tf_op | source)
XLA Modules:
  0.0 91.2 jit_solution(18079892792192870864)
XLA Ops:
  0.0 0.0 copy-start
  0.0 0.9 %copy-done = bf16[128,1024]{1,0:T(8,128)(2,1)S(1)} copy-done((bf16[128,1024]{1,0:T(8,128)(2,1)S(1)}, bf16[128,1024]{1,0:T(8,128)(2,1)}, u32[]{:S(2)}) %copy-start) | copy-done | bytes 262168
  1.0 0.0 copy-start.1
  1.0 0.9 %copy-done.1 = s32[256,256]{1,0:T(8,128)S(1)} copy-done((s32[256,256]{1,0:T(8,128)S(1)}, s32[256,256]{1,0:T(8,128)}, u32[]{:S(2)}) %copy-start.1) | copy-done | bytes 262168
  1.9 0.0 copy-start.2
  1.9 0.8 copy-done.2
  2.7 0.0 copy-start.3
  2.7 0.8 copy-done.3
  3.6 86.8 %shard_map.55 = bf16[64,4096]{1,0:T(8,128)(2,1)S(1)} custom-call(bf16[128,1024]{1,0:T(8,128)(2,1)S(1)} %copy-done, bf16[128,256]{1,0:T(8,128)(2,1)S(1)} %copy-done.2, bf16[128,256]{1,0:T(8,128)(2,1)S(1)} %copy-done.3, s32[256,256]{1,0:T(8,128)S(1)} %copy-done.1, bf16[1024,4096]{1,0:T(8,128)(2,1)} %w_hbm.1), custom_call_target="tpu_custom_call" | custom-call | tf_op jit(solution)/shard_map/pallas_call | solution.py:374
  90.4 0.8 copy.7
Async XLA Ops:
  0.0 0.9 %copy-start = (bf16[128,1024]{1,0:T(8,128)(2,1)S(1)}, bf16[128,1024]{1,0:T(8,128)(2,1)}, u32[]{:S(2)}) copy-start(bf16[128,1024]{1,0:T(8,128)(2,1)} %q_hbm.1) | copy-start | bytes 786436
  1.0 0.9 %copy-start.1 = (s32[256,256]{1,0:T(8,128)S(1)}, s32[256,256]{1,0:T(8,128)}, u32[]{:S(2)}) copy-start(s32[256,256]{1,0:T(8,128)} %mask_hbm.1) | copy-start | bytes 786436
  1.9 0.8 copy-start.2
  2.7 0.8 copy-start.3

commit v3 on v2

--- a/solution.py
+++ b/solution.py
@@ -16,7 +16,7 @@
 
 
 def kernel(q_hbm, k_hbm, v_hbm, mask_hbm, w_hbm, out_ref,
-           buf, qs, w, mask8, bias, dbias, mx, ls, acc, sbuf, att, osend, pown, psend, precv,
+           buf, kv, qs, w, mask8, bias, dbias, mx, ls, acc, sbuf, att, osend, pown, psend, precv,
            lsem, qlsem, wsem, msem, zs, zr, qss, qsr, a_s, a_r, b_s, b_r, d_s, d_r, o_s, o_r, p_s, p_r):
     s = lax.axis_index("seq")
     h = lax.axis_index("head")
@@ -66,11 +66,12 @@
         mask_hbm.at[pl.ds(pl.multiple_of((chip // 2) * 8, 8), 8)], mask8.at[0], msem.at[0])
     mask_pair = pltpu.make_async_copy(
         mask_hbm.at[pl.ds(pl.multiple_of((pair_chip // 2) * 8, 8), 8)], mask8.at[1], msem.at[1])
-    for cp in locals_:
+    stage = [pltpu.make_async_copy(k_hbm, kv.at[0], lsem.at[2]), pltpu.make_async_copy(v_hbm, kv.at[1], lsem.at[3])]
+    for cp in stage + locals_:
         cp.start()
 
     barrier = pltpu.get_barrier_semaphore()
-    friends = [a_dev(1), a_dev(-1), b_dev(1), b_dev(-1), mate, pair, across] + [
+    friends = [a_dev(1), a_dev(-1), a_dev(2), b_dev(1), b_dev(-1), mate, pair, across] + [
         dev(x, z_of(k), y, c, h) for k in (1, 2, 3)]
     for f in friends:
         pl.semaphore_signal(barrier, inc=1, device_id=f, device_id_type=MESH)
@@ -81,9 +82,8 @@
     pl.semaphore_wait(barrier, len(friends))
 
     def z_copy(k, t):
-        src = k_hbm if t == 0 else v_hbm
         zt = z_of(k)
-        return remote(src.at[:, cols((zt % 2) * 128, 128)], buf.at[c, b, z, t, a],
+        return remote(kv.at[t, :, cols((zt % 2) * 128, 128)], buf.at[c, b, z, t, a],
                       zs.at[k, t], zr.at[k, t], dev(x, zt, y, c, h))
 
     def q_copy(i):
@@ -96,10 +96,8 @@
             ref, to = buf.at[c, b, zt, :, a], a_dev(1)
         elif way == 1:
             ref, to = buf.at[c, b, zt, :, a], a_dev(-1)
-        elif way == 2:
-            ref, to = buf.at[c, b, zt, 0, (a + 3) % 4], a_dev(1)
         else:
-            ref, to = buf.at[c, b, zt, 1, (a + 1) % 4], a_dev(-1)
+            ref, to = buf.at[c, b, zt, :, a], a_dev(2)
         return remote(ref, ref, a_s.at[k, way], a_r.at[k, way], to)
 
     def b_copy(k, way):
@@ -121,6 +119,8 @@
         ref = buf.at[c, unit_of(b, i), z_of(k)]
         return remote(ref, ref, d_s.at[k, i], d_r.at[k, i], mate)
 
+    for cp in stage:
+        cp.wait()
     for k in (1, 2, 3):
         for t in range(2):
             z_copy(k, t).start()
@@ -128,8 +128,8 @@
         q_copy(i).start()
     for cp in locals_:
         cp.wait()
-    a_copy(0, 0).start()
-    a_copy(0, 1).start()
+    for way in range(3):
+        a_copy(0, way).start()
     wcopy = pltpu.make_async_copy(w_hbm, w, wsem)
     wcopy.start()
 
@@ -177,55 +177,87 @@
         return (1 - st) * (bb * 16 + zz * 4) + st * (zz * 4 + bb)
 
     def score_job(job):
-        st, bb, zz, r = job
-        rows = []
-        for i in range(4):
-            tile = (((1 - st) * (bb * 16 + zz * 4 + i) + st * (i * 16 + zz * 4 + bb)) * 2 + st) * 2
-            rows += [bias[r, tile], bias[r, tile + 1]]
-        scores = masked(dot_keys(buf[st, bb, zz, 0].reshape(512, HD), r), r, rows)
+        st, halves, r = job[0], ((job[1], job[2], 0), (job[3], job[4], job[5])), job[6]
+        rows, keys = [], []
+        for bb, zz, first in halves:
+            keys.append(buf[st, bb, zz, 0, pl.ds(first, 2)].reshape(256, HD))
+            for i in range(2):
+                tile = (((1 - st) * (bb * 16 + zz * 4 + first + i)
+                         + st * ((first + i) * 16 + zz * 4 + bb)) * 2 + st) * 2
+                rows += [bias[r, tile], bias[r, tile + 1]]
+        scores = masked(dot_keys(jnp.concatenate(keys, axis=0), r), r, rows)
         sbuf[...] = scores
         return jnp.max(scores, axis=0, keepdims=True)
 
-    def run(ks, units, streams):
-        count = len(ks) * len(units) * len(streams) * 2
-
-        def pick(values, at):
-            out = values[0]
-            for i in range(1, len(values)):
-                out = jnp.where(at == i, values[i], out)
-            return out
+    def weigh_job(job):
+        return soften(job[6], sbuf[...], job[7])
+
+    def blend_job(job, probs, shrink):
+        st = job[0]
+        vals = [buf[st, job[1], job[2], 1, 0:2].reshape(256, HD),
+                buf[st, job[3], job[4], 1, pl.ds(job[5], 2)].reshape(256, HD)]
+        blend(job[6], probs, shrink, jnp.concatenate(vals, axis=0))
+
+    def flush(job):
+        probs, shrink = weigh_job(job)
+        blend_job(job, probs, shrink)
+
+    def pick(values, at):
+        out = values[0]
+        for i in range(1, len(values)):
+            out = jnp.where(at == i, values[i], out)
+        return out
+
+    def run(units, streams, rows, pending=None):
+        count = len(units) * len(streams) * len(rows)
+
+        def parts(n):
+            u = n % len(units)
+            r = pick(rows, (n // len(units)) % len(rows))
+            other = pick(streams, n // len(units) // len(rows))
+            st = c * (1 - other) + (1 - c) * other
+            early = 1 - (x * (1 - r) + (3 - x) * r) // 2
+            base = b * (1 - other) + a * other
+
+            def place(v):
+                return unit_of(base, pick([i for _, i in units], v)), z_of(pick([k for k, _ in units], v))
+
+            here = place(u)
+            there = place(u - u % 2 + 1)
+            return st, u % 2, here, there, r, st * early
 
         def job_at(n):
-            r = n % 2
-            other = pick(streams, (n // 2) % len(streams))
-            i = pick(units, (n // 2 // len(streams)) % len(units))
-            k = pick(ks, n // 2 // len(streams) // len(units))
-            st = c * (1 - other) + (1 - c) * other
-            return st, unit_of(b * (1 - other) + a * other, i), z_of(k), r
+            st, _, here, there, r, joined = parts(n)
+            return (st, here[0], here[1], here[0] * (1 - joined) + there[0] * joined,
+                    here[1] * (1 - joined) + there[1] * joined, 2 * (1 - joined), r)
 
         ends, total = [], 0
         for n in range(count):
-            st, bb, zz, r = job_at(n)
+            st, odd, here, there, r, joined = parts(n)
             row_chip = chip * (1 - r) + pair_chip * r
-            total = total + jnp.where(first_chip(st, bb, zz) <= row_chip, 1, 0)
+            mine = jnp.where(first_chip(st, *here) <= row_chip, 1, 0)
+            other_one = jnp.where(first_chip(st, *there) <= row_chip, 1, 0)
+            use = mine * (1 - joined) + joined * (1 - odd) * jnp.maximum(mine, other_one)
+            total = total + use
             ends.append(total)
 
         def nth(t):
             n = 0
             for end in ends[:-1]:
                 n = n + jnp.where(end <= t, 1, 0)
-            return job_at(n)
-
-        @pl.when(total > 0)
-        def _():
-            def body(t, best):
-                st, bb, zz, r = nth(t)
-                probs, shrink = soften(r, sbuf[...], best)
-                following = score_job(nth(jnp.minimum(t + 1, total - 1)))
-                blend(r, probs, shrink, buf[st, bb, zz, 1].reshape(512, HD))
-                return following
-
-            lax.fori_loop(0, total, body, score_job(nth(0)))
+            return tuple(jnp.asarray(v, jnp.int32) for v in job_at(n))
+
+        def body(t, job):
+            probs, shrink = weigh_job(job)
+            following = nth(t)
+            best = score_job(following)
+            blend_job(job, probs, shrink)
+            return following + (best,)
+
+        if pending is not None:
+            return lax.fori_loop(0, total, body, pending)
+        start = nth(0)
+        return lax.fori_loop(1, total, body, start + (score_job(start),))
 
     def diagonal(r, carry):
         zz = z * (1 - r) + pair_z * r
@@ -240,21 +272,15 @@
         blend(r, probs, shrink, buf[c, bb, zz, 1, aa])
         return carry
 
-    def a_forward(k):
-        a_copy(k, 0).wait_recv()
-        a_copy(k, 2).start()
-        a_copy(k, 1).wait_recv()
-        a_copy(k, 3).start()
-
     def a_begin(k):
         z_copy(k, 0).wait_recv()
         z_copy(k, 1).wait_recv()
-        a_copy(k, 0).start()
-        a_copy(k, 1).start()
+        for way in range(3):
+            a_copy(k, way).start()
 
     def b_begin(k):
-        a_copy(k, 2).wait_recv()
-        a_copy(k, 3).wait_recv()
+        for way in range(3):
+            a_copy(k, way).wait_recv()
         b_copy(k, 0).start()
         b_copy(k, 1).start()
         d_copy(k, 0).start()
@@ -276,45 +302,57 @@
         b_copy(k, 3).wait_recv()
         d_copy(k, 3).start()
 
-    a_forward(0)
+    def own(*ks):
+        return tuple((k, 0) for k in ks)
+
+    def side(k):
+        return ((k, 1), (k, 2))
+
+    def opposite(*ks):
+        return tuple((k, 3) for k in ks)
+
     a_begin(1)
     b_begin(0)
-    a_forward(1)
     a_begin(2)
-    b_begin(1)
-    a_forward(2)
     a_begin(3)
-    b_begin(2)
     for cp in qlocals:
         cp.wait()
     for i in range(4):
         q_copy(i).wait()
-    a_forward(3)
+    b_begin(1)
+    job = run(own(0, 1), (0,), (0, 1))
+    b_begin(2)
     b_begin(3)
-    run((0, 1, 2), (0,), (0,))
-    d_arrived((0, 0), (1, 0), (2, 0), (3, 0))
+    d_arrived((0, 0), (1, 0))
+    job = run(own(0, 1), (1,), (0, 1), job)
     near(0)
-    run((0, 1, 2), (0,), (1,))
+    job = run(own(2, 3), (0,), (0, 1), job)
     near(1)
-    run((3,), (0,), (0, 1))
+    d_arrived((2, 0), (3, 0))
+    job = run(own(2, 3), (1,), (0, 1), job)
     near(2)
-    d_arrived((0, 1), (0, 2), (1, 1), (1, 2))
-    run((0, 1), (1, 2), (0, 1))
+    d_arrived((0, 1), (0, 2))
+    job = run(side(0), (0, 1), (1,), job)
     near(3)
+    lax.fori_loop(0, 2, diagonal, 0)
+    d_arrived((1, 1), (1, 2))
+    job = run(side(1), (0, 1), (1,), job)
+    job = run(side(0), (0, 1), (0,), job)
     far(0)
     d_arrived((2, 1), (2, 2))
-    run((2,), (1, 2), (0, 1))
+    job = run(side(2), (0, 1), (1,), job)
     far(1)
-    d_arrived((3, 1), (3, 2), (0, 3))
-    run((3,), (1, 2), (0, 1))
-    lax.fori_loop(0, 2, diagonal, 0)
+    d_arrived((3, 1), (3, 2))
+    job = run(side(3), (0, 1), (1,), job)
+    job = run(side(1), (0, 1), (0,), job)
     far(2)
-    d_arrived((1, 3))
-    run((0, 1), (3,), (0, 1))
+    d_arrived((0, 3), (1, 3))
+    job = run(opposite(0, 1), (0, 1), (1,), job)
     far(3)
-    run((2, 3), (3,), (0,))
+    job = run(opposite(2, 3), (0,), (1,), job)
     d_arrived((2, 3), (3, 3))
-    run((2, 3), (3,), (1,))
+    job = run(opposite(2, 3), (1,), (1,), job)
+    flush(job)
 
     def result(r):
         done = acc[r] / ls[r]
@@ -324,6 +362,8 @@
         osend[:, i * 128:(i + 1) * 128] = part
     o_copy = remote(osend, att.at[g], o_s, o_r, pair)
     o_copy.start()
+    rest = side(2) + side(3) + opposite(0, 1, 2, 3)
+    flush(run(rest, (0, 1), (0,)))
     for i, part in enumerate(result(0)):
         att[g, :, i * 128:(i + 1) * 128] = part
     wcopy.wait()
@@ -354,8 +394,9 @@
     lax.fori_loop(0, 4096 // COLS, finish, 0)
 
     def drain(k, carry):
+        for way in range(3):
+            a_copy(k, way).wait_send()
         for way in range(4):
-            a_copy(k, way).wait_send()
             b_copy(k, way).wait_send()
         for i in range(4):
             d_copy(k, i).wait_send()
@@ -378,6 +419,7 @@
         out_specs=pl.BlockSpec(memory_space=pltpu.VMEM),
         scratch_shapes=[
             pltpu.VMEM((2, 4, 4, 2, 4, 128, 128), bf),
+            pltpu.VMEM((2, 128, 256), bf),
             pltpu.VMEM((2, 4, 128, 128), bf),
             pltpu.VMEM((1024, 4096), bf),
             pltpu.VMEM((2, 8, 256), jnp.int32),
@@ -392,13 +434,13 @@
             pltpu.VMEM((n, 64, COLS), f32),
             pltpu.VMEM((n, 64, COLS), bf),
             pltpu.VMEM((n, 64, COLS), bf),
-            dma((2,)), dma((4,)), dma, dma((2,)),
+            dma((4,)), dma((4,)), dma, dma((2,)),
             dma((4, 2)), dma((4, 2)), dma((4,)), dma((4,)),
-            dma((4, 4)), dma((4, 4)), dma((4, 4)), dma((4, 4)), dma((4, 4)), dma((4, 4)),
+            dma((4, 3)), dma((4, 3)), dma((4, 4)), dma((4, 4)), dma((4, 4)), dma((4, 4)),
             dma, dma, dma((n,)), dma((n,)),
         ],
         compiler_params=pltpu.CompilerParams(
-            collective_id=0, has_side_effects=True, vmem_limit_bytes=48 * 1024 * 1024),
+            collective_id=0, has_side_effects=True, vmem_limit_bytes=67043328),
     )(queries, keys, values, tile_mask, out_weight)
 
 

time: 91.4 us -> 75.9 us (0.83)
  the two profiles are of different devices: /device:TPU:67 before, /device:TPU:71 now
where the time goes in v3:
time: 75.9 us; the launch traced here: 75.8 us
  Pallas kernels  73.9 us (97%)
  local copies, waits for them, and re-layouts  1.87 us (2%)
    pallas_call x1, Pallas kernels, per_device(): pl.pallas_call(kernel, out_shape=jax.ShapeDtypeStruct((64, 4096), bf), in...  73.9 us
    unnamed x1, local copies, waits for them, and re-layouts  1.87 us

profile of v3, /device:TPU:71, one launch (start us, length us, event | category | flops | bytes accessed | tf_op | source)
XLA Modules:
  0.0 75.8 jit_solution(2256571334353596257)
XLA Ops:
  0.0 73.9 %shard_map.55 = bf16[64,4096]{1,0:T(8,128)(2,1)} custom-call(bf16[128,1024]{1,0:T(8,128)(2,1)} %q_hbm.1, bf16[128,256]{1,0:T(8,128)(2,1)} %k_hbm.1, bf16[128,256]{1,0:T(8,128)(2,1)} %v_hbm.1, s32[256,256]{1,0:T(8,128)} %mask_hbm.1, bf16[1024,4096]{1,0:T(8,128)(2,1)} %w_hbm.1), custom_call_target="tpu_custom_call" | custom-call | tf_op jit(solution)/shard_map/pallas_call | solution.py:415
  73.9 1.9 %copy.7 = bf16[64,4096]{1,0:T(8,128)(2,1)} copy(bf16[64,4096]{1,0:T(8,128)(2,1)} %shard_map.55) | data formatting | bytes 1048576

commit v4 on v3

--- a/solution.py
+++ b/solution.py
@@ -16,8 +16,9 @@
 
 
 def kernel(q_hbm, k_hbm, v_hbm, mask_hbm, w_hbm, out_ref,
-           buf, kv, qs, w, mask8, bias, dbias, mx, ls, acc, sbuf, att, osend, pown, psend, precv,
-           lsem, qlsem, wsem, msem, zs, zr, qss, qsr, a_s, a_r, b_s, b_r, d_s, d_r, o_s, o_r, p_s, p_r):
+           buf, kv, qs, w, wo, mask8, bias, dbias, mx, ls, acc, sbuf, att, attx, osend, tot,
+           lsem, qlsem, wsem, msem, zs, zr, qss, qsr, a_s, a_r, b_s, b_r, d_s, d_r, o_s, o_r,
+           wf_s, wf_r, wa_s, wa_r, wb_s, wb_r, wg_s, wg_r, wd_s, wd_r, wh_s, wh_r, x_s, x_r):
     s = lax.axis_index("seq")
     h = lax.axis_index("head")
     c = s % 2
@@ -119,6 +120,38 @@
         ref = buf.at[c, unit_of(b, i), z_of(k)]
         return remote(ref, ref, d_s.at[k, i], d_r.at[k, i], mate)
 
+    def wf_copy(i):
+        slot = (a + 2 * i) % 4
+        row = pl.multiple_of(((c * 4 + b) * 4 + slot) * 32, 32)
+        return remote(w_hbm.at[pl.ds(row, 32)], wo.at[c, b, slot], wf_s.at[i], wf_r.at[i], across)
+
+    def wa_copy(way):
+        ref = wo.at[c, b, a]
+        return remote(ref, ref, wa_s.at[way], wa_r.at[way], a_dev(1 - 2 * way))
+
+    def slot_of(j):
+        return (a + (0, 3, 1, 2)[j]) % 4
+
+    def wb_copy(way, j):
+        ref = wo.at[c, b, slot_of(j)]
+        return remote(ref, ref, wb_s.at[way, j], wb_r.at[way, j], b_dev(1 - 2 * way))
+
+    def wg_copy(j):
+        ref = wo.at[c, (b + (3, 3, 1, 1)[j]) % 4, slot_of(j)]
+        return remote(ref, ref, wg_s.at[j], wg_r.at[j], b_dev((1, 1, -1, -1)[j]))
+
+    def wh_copy(j):
+        ref = wo.at[c, (b + 2) % 4, slot_of(j)]
+        return remote(ref, ref, wh_s.at[j], wh_r.at[j], mate)
+
+    def w_forward(j):
+        wb_copy((0, 0, 1, 1)[j], j).wait_recv()
+        wg_copy(j).start()
+
+    def wd_copy(i):
+        ref = wo.at[c, unit_of(b, i)]
+        return remote(ref, ref, wd_s.at[i], wd_r.at[i], mate)
+
     for cp in stage:
         cp.wait()
     for k in (1, 2, 3):
@@ -126,6 +159,7 @@
             z_copy(k, t).start()
     for i in range(4):
         q_copy(i).start()
+    wf_copy(0).start()
     for cp in locals_:
         cp.wait()
     for way in range(3):
@@ -326,6 +360,7 @@
     d_arrived((0, 0), (1, 0))
     job = run(own(0, 1), (1,), (0, 1), job)
     near(0)
+    wf_copy(1).start()
     job = run(own(2, 3), (0,), (0, 1), job)
     near(1)
     d_arrived((2, 0), (3, 0))
@@ -334,6 +369,10 @@
     d_arrived((0, 1), (0, 2))
     job = run(side(0), (0, 1), (1,), job)
     near(3)
+    wf_copy(0).wait_recv()
+    for way in range(2):
+        wa_copy(way).start()
+        wb_copy(way, 0).start()
     lax.fori_loop(0, 2, diagonal, 0)
     d_arrived((1, 1), (1, 2))
     job = run(side(1), (0, 1), (1,), job)
@@ -346,9 +385,20 @@
     job = run(side(3), (0, 1), (1,), job)
     job = run(side(1), (0, 1), (0,), job)
     far(2)
+    for way in range(2):
+        wa_copy(way).wait_recv()
+    for j in (1, 2):
+        for way in range(2):
+            wb_copy(way, j).start()
     d_arrived((0, 3), (1, 3))
     job = run(opposite(0, 1), (0, 1), (1,), job)
+    job = run(side(2), (0, 1), (0,), job)
     far(3)
+    wf_copy(1).wait_recv()
+    for way in range(2):
+        wb_copy(way, 3).start()
+    wd_copy(0).start()
+    w_forward(0)
     job = run(opposite(2, 3), (0,), (1,), job)
     d_arrived((2, 3), (3, 3))
     job = run(opposite(2, 3), (1,), (1,), job)
@@ -362,36 +412,67 @@
         osend[:, i * 128:(i + 1) * 128] = part
     o_copy = remote(osend, att.at[g], o_s, o_r, pair)
     o_copy.start()
-    rest = side(2) + side(3) + opposite(0, 1, 2, 3)
-    flush(run(rest, (0, 1), (0,)))
+    w_forward(1)
+    job = run(side(3), (0, 1), (0,))
+    w_forward(2)
+    flush(run(opposite(0, 1, 2, 3), (0, 1), (0,), job))
     for i, part in enumerate(result(0)):
         att[g, :, i * 128:(i + 1) * 128] = part
     wcopy.wait()
     o_copy.wait()
 
-    def p_copy(n):
-        return remote(psend.at[n], precv.at[n], p_s.at[n], p_r.at[n], across)
+    x_copy = remote(att.at[:, pl.ds(pl.multiple_of((1 - h) * 64, 64), 64)], attx, x_s, x_r, across)
+    x_copy.start()
+    w_forward(3)
+    for j in range(4):
+        wb_copy((1, 1, 0, 0)[j], j).wait_recv()
+    wd_copy(1).start()
+    wd_copy(2).start()
+    mine = [jnp.where(h == 0, att[i, 0:64], att[i, 64:128]) for i in range(2)]
 
     def project(n, carry):
         at = cols(n * COLS, COLS)
-        part = jnp.dot(att[0], w[0:512, at], preferred_element_type=jnp.float32)
-        part = part + jnp.dot(att[1], w[512:1024, at], preferred_element_type=jnp.float32)
-        upper, lower = part[0:64], part[64:128]
-        mine = jnp.where(h == 0, upper, lower)
-        theirs = jnp.where(h == 0, lower, upper)
-        psend[n] = theirs.astype(jnp.bfloat16)
-        p_copy(n).start()
-        pown[n] = mine
+        part = jnp.dot(mine[0], w[0:512, at], preferred_element_type=jnp.float32)
+        tot[:, at] = part + jnp.dot(mine[1], w[512:1024, at], preferred_element_type=jnp.float32)
         return carry
 
     lax.fori_loop(0, 4096 // COLS, project, 0)
 
-    def finish(n, carry):
-        p_copy(n).wait()
-        out_ref[:, cols(n * COLS, COLS)] = (pown[n] + precv[n].astype(jnp.float32)).astype(jnp.bfloat16)
+    for j in range(3):
+        wg_copy(j).wait_recv()
+        wh_copy(j).start()
+    x_copy.wait()
+
+    def share(i, at):
+        left, right = [], []
+        for st in range(2):
+            base = b * (1 - c) + a * c if st == 0 else b * c + a * (1 - c)
+            bb = unit_of(base, i)
+            left.append(attx[st, :, cols(bb * 128, 128)])
+            right.append(wo[st, bb, :, :, at].reshape(128, COLS))
+        return jnp.dot(jnp.concatenate(left, axis=1), jnp.concatenate(right, axis=0),
+                       preferred_element_type=jnp.float32)
+
+    for i in range(3):
+        wd_copy(i).wait_recv()
+
+    def project_near(n, carry):
+        at = cols(n * COLS, COLS)
+        tot[:, at] = tot[:, at] + (share(0, at) + share(1, at) + share(2, at))
         return carry
 
-    lax.fori_loop(0, 4096 // COLS, finish, 0)
+    lax.fori_loop(0, 4096 // COLS, project_near, 0)
+    wg_copy(3).wait_recv()
+    wh_copy(3).start()
+    for j in range(4):
+        wh_copy(j).wait_recv()
+
+    def project_far(n, carry):
+        at = cols(n * COLS, COLS)
+        out_ref[:, at] = (tot[:, at] + share(3, at)).astype(jnp.bfloat16)
+        return carry
+
+    lax.fori_loop(0, 4096 // COLS, project_far, 0)
 
     def drain(k, carry):
         for way in range(3):
@@ -406,12 +487,21 @@
     for k in (1, 2, 3):
         for t in range(2):
             z_copy(k, t).wait_send()
+    for way in range(2):
+        wf_copy(way).wait_send()
+        wa_copy(way).wait_send()
+        for j in range(4):
+            wb_copy(way, j).wait_send()
+    for i in range(3):
+        wd_copy(i).wait_send()
+    for j in range(4):
+        wg_copy(j).wait_send()
+        wh_copy(j).wait_send()
 
 
 def per_device(queries, keys, values, tile_mask, out_weight):
     dma = pltpu.SemaphoreType.DMA
     bf, f32 = jnp.bfloat16, jnp.float32
-    n = 4096 // COLS
     return pl.pallas_call(
         kernel,
         out_shape=jax.ShapeDtypeStruct((64, 4096), bf),
@@ -422,6 +512,7 @@
             pltpu.VMEM((2, 128, 256), bf),
             pltpu.VMEM((2, 4, 128, 128), bf),
             pltpu.VMEM((1024, 4096), bf),
+            pltpu.VMEM((2, 4, 4, 32, 4096), bf),
             pltpu.VMEM((2, 8, 256), jnp.int32),
             pltpu.VMEM((2, 256, 1, 128), f32),
             pltpu.VMEM((2, 2, 1, 128), f32),
@@ -430,14 +521,14 @@
             pltpu.VMEM((2, 128, 512), f32),
             pltpu.VMEM((512, 512), f32),
             pltpu.VMEM((2, 128, 512), bf),
+            pltpu.VMEM((2, 64, 512), bf),
             pltpu.VMEM((128, 512), bf),
-            pltpu.VMEM((n, 64, COLS), f32),
-            pltpu.VMEM((n, 64, COLS), bf),
-            pltpu.VMEM((n, 64, COLS), bf),
+            pltpu.VMEM((64, 4096), f32),
             dma((4,)), dma((4,)), dma, dma((2,)),
             dma((4, 2)), dma((4, 2)), dma((4,)), dma((4,)),
             dma((4, 3)), dma((4, 3)), dma((4, 4)), dma((4, 4)), dma((4, 4)), dma((4, 4)),
-            dma, dma, dma((n,)), dma((n,)),
+            dma, dma, dma((2,)), dma((2,)), dma((2,)), dma((2,)), dma((2, 4)), dma((2, 4)),
+            dma((4,)), dma((4,)), dma((3,)), dma((3,)), dma((4,)), dma((4,)), dma, dma,
         ],
         compiler_params=pltpu.CompilerParams(
             collective_id=0, has_side_effects=True, vmem_limit_bytes=67043328),

time: 75.9 us -> 71.4 us (0.941); the launches traced: 75.8 us -> 70.3 us
  Pallas kernels: 73.9 us -> 68.4 us
    pallas_call x1, Pallas kernels: 73.9 us -> 68.4 us  [per_device(): pl.pallas_call(kernel, out_shape=jax.ShapeDtypeStruct((64, 4096), bf), in...]
where the time goes in v4:
time: 71.4 us; the launch traced here: 70.3 us
  Pallas kernels  68.4 us (96%)
  local copies, waits for them, and re-layouts  1.87 us (3%)
    pallas_call x1, Pallas kernels, per_device(): pl.pallas_call(kernel, out_shape=jax.ShapeDtypeStruct((64, 4096), bf), in...  68.4 us
    unnamed x1, local copies, waits for them, and re-layouts  1.87 us

profile of v4, /device:TPU:71, one launch (start us, length us, event | category | flops | bytes accessed | tf_op | source)
XLA Modules:
  0.0 70.3 jit_solution(1228069366579862520)
XLA Ops:
  0.0 68.4 %shard_map.55 = bf16[64,4096]{1,0:T(8,128)(2,1)} custom-call(bf16[128,1024]{1,0:T(8,128)(2,1)} %q_hbm.1, bf16[128,256]{1,0:T(8,128)(2,1)} %k_hbm.1, bf16[128,256]{1,0:T(8,128)(2,1)} %v_hbm.1, s32[256,256]{1,0:T(8,128)} %mask_hbm.1, bf16[1024,4096]{1,0:T(8,128)(2,1)} %w_hbm.1), custom_call_target="tpu_custom_call" | custom-call | tf_op jit(solution)/shard_map/pallas_call | solution.py:505
  68.4 1.9 %copy.7 = bf16[64,4096]{1,0:T(8,128)(2,1)} copy(bf16[64,4096]{1,0:T(8,128)(2,1)} %shard_map.55) | data formatting | bytes 1048576

commit v5 on v4

--- a/solution.py
+++ b/solution.py
@@ -351,6 +351,7 @@
     a_begin(3)
     for cp in qlocals:
         cp.wait()
+    diagonal(0, 0)
     for i in range(4):
         q_copy(i).wait()
     b_begin(1)
@@ -373,7 +374,7 @@
     for way in range(2):
         wa_copy(way).start()
         wb_copy(way, 0).start()
-    lax.fori_loop(0, 2, diagonal, 0)
+    diagonal(1, 0)
     d_arrived((1, 1), (1, 2))
     job = run(side(1), (0, 1), (1,), job)
     job = run(side(0), (0, 1), (0,), job)
@@ -412,9 +413,7 @@
         osend[:, i * 128:(i + 1) * 128] = part
     o_copy = remote(osend, att.at[g], o_s, o_r, pair)
     o_copy.start()
-    w_forward(1)
     job = run(side(3), (0, 1), (0,))
-    w_forward(2)
     flush(run(opposite(0, 1, 2, 3), (0, 1), (0,), job))
     for i, part in enumerate(result(0)):
         att[g, :, i * 128:(i + 1) * 128] = part
@@ -423,6 +422,8 @@
 
     x_copy = remote(att.at[:, pl.ds(pl.multiple_of((1 - h) * 64, 64), 64)], attx, x_s, x_r, across)
     x_copy.start()
+    w_forward(1)
+    w_forward(2)
     w_forward(3)
     for j in range(4):
         wb_copy((1, 1, 0, 0)[j], j).wait_recv()

time: 71.4 us -> 71.4 us (level)
  the two profiles are of different devices: /device:TPU:71 before, /device:TPU:1 now
where the time goes in v5:
time: 71.4 us; the launch traced here: 71.3 us
  Pallas kernels  69.4 us (97%)
  local copies, waits for them, and re-layouts  1.87 us (3%)
    pallas_call x1, Pallas kernels, per_device(): pl.pallas_call(kernel, out_shape=jax.ShapeDtypeStruct((64, 4096), bf), in...  69.4 us
    unnamed x1, local copies, waits for them, and re-layouts  1.87 us

profile of v5, /device:TPU:1, one launch (start us, length us, event | category | flops | bytes accessed | tf_op | source)
XLA Modules:
  0.0 71.3 jit_solution(12274959608613754478)
XLA Ops:
  0.0 69.4 %shard_map.55 = bf16[64,4096]{1,0:T(8,128)(2,1)} custom-call(bf16[128,1024]{1,0:T(8,128)(2,1)} %q_hbm.1, bf16[128,256]{1,0:T(8,128)(2,1)} %k_hbm.1, bf16[128,256]{1,0:T(8,128)(2,1)} %v_hbm.1, s32[256,256]{1,0:T(8,128)} %mask_hbm.1, bf16[1024,4096]{1,0:T(8,128)(2,1)} %w_hbm.1), custom_call_target="tpu_custom_call" | custom-call | tf_op jit(solution)/shard_map/pallas_call | solution.py:506
  69.4 1.9 %copy.7 = bf16[64,4096]{1,0:T(8,128)(2,1)} copy(bf16[64,4096]{1,0:T(8,128)(2,1)} %shard_map.55) | data formatting | bytes 1048576
